TPU v7x, 32 devices: a whole 2x2x4 slice. The times are simulated.
32 devices in a mesh: src: 8 (over z, y), reg: 4 (over x, core).
Axes of the slice: x: 2, y: 2, z: 4, core: 2. Of those that a mesh axis runs over, the one named last changes fastest.
Arguments:
- tiles: bfloat16 [16384, 128, 128], P(('src', 'reg')), may hold values from -0.1875 to 0.1875
- rays: float32 [2048, 128], P(('src', 'reg')), may hold values from -6 to 6
- tile_rows: int32 [16384], P(('src', 'reg')), may hold values from 0 to 63, as said below
- tile_slots: int32 [16384], P(('src', 'reg')), may hold values from 0 to 63, as said below
- tile_count: int32 [32], P(('src', 'reg')), may hold values from 64 to 512, as said below
- wanted: int32 [32, 32, 2], P(('src', 'reg')), may hold values from 0 to 255
Outputs:
- solution: float32 [8192, 128], P(('src', 'reg'))
- right_vector: float32 [8192, 128], P(('src', 'reg'))
Inputs may be any that keep to these rules, and one draw needn't show every extreme that they name: `tile_rows`: non-decreasing along each device's 512 tiles. `tile_slots`: the first 64 tiles of each device name every slot once. `tile_count`: some device has all 512 tiles live.
All inputs are finite; a program needn't handle non-finite values.
Results may differ from a plain program's by a relative error of at most 0.024.
Values may be sent and summed in bfloat16 or wider, within the bound.
A program may use at most 128 MiB of HBM per device.

v0:
```python
import functools

import jax
import jax.numpy as jnp
from jax import lax
from jax.experimental import pallas as pl
from jax.experimental.pallas import tpu as pltpu
from jax.sharding import PartitionSpec as P

BLK_DEV = 256
ITERS = 3
damping = 0.5

GROUP = 16
HALF = GROUP // 2
F32 = jnp.float32
BF16 = jnp.bfloat16
MESH = pl.DeviceIdType.MESH


def one_hot_dot(hot, x, parts=2):
    total = None
    for part in range(parts):
        piece = x.astype(BF16)
        prod = jnp.dot(hot, piece, preferred_element_type=F32)
        total = prod if total is None else total + prod
        if part < parts - 1:
            x = x - piece.astype(F32)
    return total


def kernel(
    n, regs, stride, cap, chunks,
    count_ref, tiles_hbm, rays_ref, rows_ref, slots_ref, wanted_ref,
    sol_ref, right_ref,
    tiles_ref, turned_ref, left_ref, mid_ref, slot_hot, slot_hot_t, ray_hot, ray_hot_t, same_ref,
    send_ref, recv_ref, tile_sem, send_sem, recv_sem,
):
    src = lax.axis_index("src")
    reg = lax.axis_index("reg")
    me = src * regs + reg
    count = tiles_ref.shape[0]
    width = tiles_ref.shape[2]
    per_chunk = count // chunks
    groups = count // GROUP
    rows = n * stride
    row_blocks = rays_ref.shape[0]

    def tile_copy(c):
        part = pl.ds(c * per_chunk, per_chunk)
        return pltpu.make_async_copy(tiles_hbm.at[part], tiles_ref.at[part], tile_sem.at[c])

    for c in range(chunks):
        tile_copy(c).start()

    barrier = pltpu.get_barrier_semaphore()

    @pl.loop(1, n)
    def _(k):
        d = lax.rem(me + k, n)
        pl.semaphore_signal(
            barrier, inc=1, device_id=(d // regs, lax.rem(d, regs)), device_id_type=MESH
        )

    def hot(a, b):
        return jnp.where(a == b, 1.0, 0.0).astype(BF16)

    iota = functools.partial(lax.broadcasted_iota, jnp.int32)
    live = iota((1, count), 1) < count_ref[0]
    slots = slots_ref[...]
    slots = jnp.where(live, slots // cap * stride + lax.rem(slots, cap), -1)
    one_slot = hot(iota((rows, count), 0), slots)
    one_ray = hot(iota((row_blocks, count), 0), jnp.where(live, rows_ref[...], -1))
    slot_hot[...] = one_slot
    slot_hot_t[...] = one_slot.T
    ray_hot[...] = one_ray
    ray_hot_t[...] = one_ray.T
    wanted = wanted_ref[...].astype(F32)
    row_place = lax.rem(iota((1, rows), 1), stride)
    col_place = lax.rem(iota((rows, 1), 0), stride)
    peers_t = jnp.where(iota((n, rows), 0) == iota((n, rows), 1) // stride, 1.0, 0.0)
    peers = jnp.where(iota((rows, n), 1) == iota((rows, n), 0) // stride, 1.0, 0.0)
    req_row = jnp.where(row_place < cap, 0.0, -1.0)
    req_col = jnp.where(col_place < cap, 0.0, -1.0)
    for k in range(cap):
        asked = wanted[k : k + 1, :]
        req_col += jnp.where(col_place == k, jnp.sum(peers * asked, axis=1, keepdims=True), 0.0)
        picked = jnp.dot(
            jnp.broadcast_to(asked, (8, n)), peers_t, preferred_element_type=F32,
            precision=lax.Precision.HIGHEST,
        )[:1]
        req_row += jnp.where(row_place == k, picked, 0.0)
    same = (req_col == req_row) & (req_col >= 0.0)
    same_ref[...] = jnp.where(same, 1.0, 0.0).astype(BF16)
    lower = jnp.where(same & (iota((rows, rows), 1) < iota((rows, rows), 0)), 1.0, 0.0)
    upper = jnp.where(same & (iota((rows, rows), 0) < iota((rows, rows), 1)), 1.0, 0.0)
    first_col = jnp.where(jnp.sum(lower, axis=1, keepdims=True) == 0.0, 1.0, 0.0)
    first_row = jnp.where(jnp.sum(upper, axis=0, keepdims=True) == 0.0, 1.0, 0.0)
    place = lax.rem(iota((rows, width), 0), stride)
    is_high = place == cap
    is_low = place == cap + 1
    is_sum = is_high | is_low

    def packed(value, squares):
        high = squares.astype(BF16).astype(F32)
        value = jnp.where(is_high, high, value)
        return jnp.where(is_low, squares - high, value).astype(BF16)


    spot = lax.rem(iota((GROUP, width), 0), HALF)
    masks = [jnp.where(spot == b, 1.0, 0.0).astype(BF16) for b in range(HALF)]

    def spread(g):
        base = pl.multiple_of(g * GROUP, GROUP)
        left = left_ref[pl.ds(base, GROUP), :]
        return base, jnp.concatenate([left * m for m in masks], axis=1)

    def keep(base, out):
        mid_ref[pl.ds(base, HALF), :] = out[:HALF, :width]
        mid_ref[pl.ds(pl.multiple_of(base + HALF, HALF), HALF), :] = out[HALF:, width:]

    def group(source, g):
        base, left = spread(g)
        a = source[pl.ds(base, HALF)].reshape(HALF * width, width)
        b = source[pl.ds(base + HALF, HALF)].reshape(HALF * width, width)
        right = jnp.concatenate([a, b], axis=1)
        keep(base, jnp.dot(left, right, preferred_element_type=F32))

    upper_half = me >= n // 2
    skip = jnp.where(upper_half, me, n - 1 - me)

    def exchange(phase, value):
        send_ref[phase] = value.reshape(n, stride, width)

        @pl.loop(0, n - 1)
        def _(j):
            j = j + jnp.where(j >= skip, 1, 0)
            d = jnp.where(upper_half, j, n - 1 - j)
            pltpu.make_async_remote_copy(
                src_ref=send_ref.at[phase, d],
                dst_ref=recv_ref.at[phase, me],
                send_sem=send_sem.at[phase],
                recv_sem=recv_sem.at[phase],
                device_id=(d // regs, lax.rem(d, regs)),
                device_id_type=MESH,
            ).start()

        recv_ref[phase, me] = send_ref[phase, me]
        others = pl.ds(0, n - 1)
        pltpu.make_async_copy(
            recv_ref.at[phase, others], recv_ref.at[phase, others], recv_sem.at[phase]
        ).wait()
        got = recv_ref[phase].reshape(rows, width)
        return got, jnp.sum(
            jnp.where(is_sum, got.astype(F32), 0.0), keepdims=True
        )

    uraw = rays_ref[...]
    u = None
    v = w = update = jnp.zeros((rows, width), F32)
    alpha = phibar = rhobar = None
    fetched = None
    for step in range(ITERS + 1):
        if step > 0:
            left_ref[...] = jnp.dot(
                slot_hot_t[...], fetched, preferred_element_type=F32
            ).astype(BF16)

            @pl.loop(0, groups, unroll=2)
            def _(g):
                group(turned_ref, g)

            uraw = one_hot_dot(ray_hot[...], mid_ref[...]) / alpha - alpha * u
        left_ref[...] = jnp.dot(
            ray_hot_t[...], uraw.astype(BF16), preferred_element_type=F32
        ).astype(BF16)
        if step == 0:
            per = groups // chunks

            @pl.loop(0, chunks)
            def _(c):
                tile_copy(c).wait()
                for i in range(per):
                    group(tiles_ref, c * per + i)

                for i in range(per_chunk):
                    t = c * per_chunk + i
                    turned_ref[t] = tiles_ref[t].T
        else:

            @pl.loop(0, groups, unroll=2)
            def _(g):
                group(tiles_ref, g)

        sums = one_hot_dot(slot_hot[...], mid_ref[...])
        squares = jnp.sum(uraw * uraw, axis=0, keepdims=True)
        if step == 0:
            pl.semaphore_wait(barrier, n - 1)
        got, uu = exchange(2 * step, packed(sums, squares))
        beta = jnp.sqrt(uu)
        u = uraw / beta
        vraw = jnp.dot(same_ref[...], got, preferred_element_type=F32) / beta
        if step > 0:
            vraw = vraw - beta * v
        squares = jnp.sum(vraw * vraw * first_col, axis=0, keepdims=True)
        fetched, vv = exchange(2 * step + 1, packed(vraw, squares))
        alpha = jnp.sqrt(vv)
        v = jnp.where(place < cap, vraw, 0.0) / alpha
        if step == 0:
            w = v
            phibar = beta
            rhobar = alpha
        else:
            rhobar1 = jnp.sqrt(rhobar * rhobar + damping * damping)
            phibar = rhobar / rhobar1 * phibar
            rho = jnp.sqrt(rhobar1 * rhobar1 + beta * beta)
            cosine = rhobar1 / rho
            sine = beta / rho
            theta = sine * alpha
            rhobar = -cosine * alpha
            phi = cosine * phibar
            phibar = sine * phibar
            update = update + phi / rho * w
            w = v - theta / rho * w
    blocks = sol_ref.shape[0]
    out_hot = jnp.where(
        iota((blocks, rows), 0).astype(F32) == req_row, first_row, 0.0
    ).astype(BF16)
    scale = float(blocks * width * n) ** 0.5
    sol_ref[...] = one_hot_dot(out_hot, update, 3)
    right_ref[...] = one_hot_dot(out_hot, v * scale, 3)
    for phase in range(2 * (ITERS + 1)):
        others = pl.ds(0, n - 1)
        pltpu.make_async_copy(
            send_ref.at[phase, others], send_ref.at[phase, others], send_sem.at[phase]
        ).wait()


def per_device(n, regs, tiles, rays, tile_rows, tile_slots, tile_count, wanted):
    count, width = tiles.shape[0], tiles.shape[2]
    cap = wanted.shape[2]
    stride = 4
    while stride < cap + 2:
        stride *= 2
    rows = n * stride
    chunks = 16
    phases = 2 * (ITERS + 1)
    row_blocks = rays.shape[0]
    vmem = pl.BlockSpec(memory_space=pltpu.VMEM)
    out = jax.ShapeDtypeStruct((BLK_DEV, width), F32)
    return pl.pallas_call(
        functools.partial(kernel, n, regs, stride, cap, chunks),
        out_shape=(out, out),
        in_specs=[
            pl.BlockSpec(memory_space=pltpu.SMEM),
            pl.BlockSpec(memory_space=pl.ANY),
        ]
        + [vmem] * 4,
        out_specs=(vmem, vmem),
        scratch_shapes=[
            pltpu.VMEM(tiles.shape, BF16),
            pltpu.VMEM(tiles.shape, BF16),
            pltpu.VMEM((count, width), BF16),
            pltpu.VMEM((count, width), F32),
            pltpu.VMEM((rows, count), BF16),
            pltpu.VMEM((count, rows), BF16),
            pltpu.VMEM((row_blocks, count), BF16),
            pltpu.VMEM((count, row_blocks), BF16),
            pltpu.VMEM((rows, rows), BF16),
            pltpu.VMEM((phases, n, stride, width), BF16),
            pltpu.VMEM((phases, n, stride, width), BF16),
            pltpu.SemaphoreType.DMA((chunks,)),
            pltpu.SemaphoreType.DMA((phases,)),
            pltpu.SemaphoreType.DMA((phases,)),
        ],
        compiler_params=pltpu.CompilerParams(
            collective_id=0, has_side_effects=True, vmem_limit_bytes=56 * 1024 * 1024
        ),
    )(
        tile_count,
        tiles,
        rays,
        tile_rows[None, :],
        tile_slots[None, :],
        wanted[0].T,
    )


def solution(mesh):
    both = ("src", "reg")
    in_specs = (
        P(both, None, None),
        P(both, None),
        P(both),
        P(both),
        P(both),
        P(both, None, None),
    )
    out_specs = (P(both, None), P(both, None))
    n = mesh.shape["src"] * mesh.shape["reg"]
    return jax.shard_map(
        functools.partial(per_device, n, mesh.shape["reg"]),
        mesh=mesh,
        in_specs=in_specs,
        out_specs=out_specs,
        check_vma=False,
    )
```

profile of v0, /device:TPU:0, one launch (start us, length us, event | category | flops | bytes accessed | tf_op | source)
XLA Modules:
  0.0 79.3 jit_solution(1373161553253514144)
XLA Ops:
  1.3 74.9 %shard_map.77 = (f32[256,128]{1,0:T(8,128)}, f32[256,128]{1,0:T(8,128)}) custom-call(s32[1]{0:T(128)S(6)} %copy.10.count_ref, bf16[512,128,128]{2,1,0:T(8,128)(2,1)} %tiles_hbm.1, f32[64,128]{1,0:T(8,128)} %rays_ref.1, s32[1,512]{1,0:T(1,128)} %bitcast.5, s32[1,512]{1,0:T(1,128)} %bitcast.6, s32[2,32]{1,0:T(2,128)} %bitcast.7), custom_call_target="tpu_custom_call" | custom-call | tf_op jit(solution)/shard_map/pallas_call | solution.py:251
  76.2 1.6 %copy.11 = f32[256,128]{1,0:T(8,128)} copy(f32[256,128]{1,0:T(8,128)} %get-tuple-element.4) | data formatting | bytes 262144
  77.7 1.6 %copy.12 = f32[256,128]{1,0:T(8,128)} copy(f32[256,128]{1,0:T(8,128)} %get-tuple-element.5) | data formatting | bytes 262144
where the time goes:
time: 79.5 us; the launch traced here: 79.3 us
  Pallas kernels  74.9 us (94%)
  local copies, waits for them, and re-layouts  3.14 us (4%)
  between operations  1.29 us (2%)
    pallas_call x1, Pallas kernels, per_device(): pl.pallas_call(functools.partial(kernel, n, regs, stride, cap, chunks), o...  74.9 us
    unnamed x2, local copies, waits for them, and re-layouts  3.14 us

commit v1 on v0

v1 whole, which is shorter than its diff:
```python
import functools

import jax
import jax.numpy as jnp
from jax import lax
from jax.experimental import pallas as pl
from jax.experimental.pallas import tpu as pltpu
from jax.sharding import PartitionSpec as P

BLK_DEV = 256
ITERS = 3
damping = 0.5

QUARTERS = 4
CHUNKS = 16
F32 = jnp.float32
BF16 = jnp.bfloat16
MESH = pl.DeviceIdType.MESH
SIDE = 256


def kernel(
    n, regs, cap,
    count_ref, tiles_hbm, rays_ref, rows_ref, slots_ref, wanted_ref,
    sol_ref, right_ref,
    tiles_ref, turned_ref, index_vec, index_ref, goes_vec, goes_ref, plain_ref, ray_ref, cell_ref,
    key_send, key_recv, key_rows, same_ref, out_hot, inv_ref,
    vraw_ref, w_ref, update_ref, final_ref, final_recv,
    send_a, recv_a, norm_a, norm_recv_a, send_b, recv_b, norm_b, norm_recv_b,
    tile_sem, index_sem, send_sem, key_sem, a_sem, na_sem, b_sem, nb_sem, final_sem,
    acc_ray, acc_cell, acc_sum,
):
    src = lax.axis_index("src")
    reg = lax.axis_index("reg")
    me = src * regs + reg
    count = tiles_ref.shape[0]
    width = tiles_ref.shape[2]
    per_chunk = count // CHUNKS
    row_blocks = rays_ref.shape[0]
    steps = ITERS + 1
    chips = n // 2
    group = n // QUARTERS
    reducers = group // 2
    part = 2 * QUARTERS * cap
    slots_all = n * cap
    asked = n * part
    chip = me // 2
    core = lax.rem(me, 2)
    quarter = me // group
    place = lax.rem(chip, reducers)
    is_reducer = core == 1
    is_other = core == 0
    iota = functools.partial(lax.broadcasted_iota, jnp.int32)

    def tile_copy(c):
        span = pl.ds(c * per_chunk, per_chunk)
        return pltpu.make_async_copy(tiles_hbm.at[span], tiles_ref.at[span], tile_sem.at[c])

    for c in range(CHUNKS):
        tile_copy(c).start()

    def at(d):
        return (d // regs, lax.rem(d, regs))

    barrier = pltpu.get_barrier_semaphore()

    def greet(d):
        pl.semaphore_signal(barrier, inc=1, device_id=at(d), device_id_type=MESH)

    @pl.loop(1, chips)
    def _(k):
        greet(lax.rem(chip + k, chips) * 2 + 1)

    @pl.when(is_reducer)
    def _():
        @pl.loop(0, chips)
        def _(k):
            greet(lax.rem(chip + k, chips) * 2)

    @pl.when(is_other)
    def _():
        greet(me + 1)

    lines = rows_ref.shape[0]
    tile_id = iota((lines, width), 0) * width + iota((lines, width), 1)
    live = tile_id < count_ref[...]
    slots = slots_ref[...]
    owner = slots // cap
    within = lax.rem(owner, group)
    spot = (within // 2) * part + (2 * (owner // group) + lax.rem(within, 2)) * cap + lax.rem(slots, cap)
    index_vec[:lines, :] = jnp.where(live, rows_ref[...], row_blocks)
    index_vec[lines:, :] = jnp.where(live, spot, slots_all)
    goes_vec[...] = index_vec[...].astype(F32)
    index_copies = (
        pltpu.make_async_copy(index_vec, index_ref, index_sem.at[0]),
        pltpu.make_async_copy(goes_vec, goes_ref, index_sem.at[1]),
    )
    for copy in index_copies:
        copy.start()

    asks = wanted_ref[...].astype(F32)
    lane = iota((1, asked), 1)
    asker = iota((cap, asked), 1) // part
    spread = jnp.zeros((cap, asked), F32)
    for d in range(n):
        spread = jnp.where(asker == d, asks[:, d : d + 1], spread)
    which = 2 * quarter + core
    keys = jnp.zeros((1, asked), F32)
    for k in range(cap):
        hit = lax.rem(lane, part) == which * cap + k
        keys = keys + jnp.where(hit, spread[k : k + 1] + (which * BLK_DEV).astype(F32), 0.0)
    key_send[...] = keys

    for acc in (*acc_ray, *acc_cell, *acc_sum):
        pltpu.matmul_pop(acc)

    ray_ref[row_blocks] = jnp.zeros((16, width), BF16)
    cell_ref[slots_all] = jnp.zeros((16, width), BF16)

    def spread_rows(vec_ref, value):
        plain_ref[pl.ds(0, value.shape[0]), :] = value
        for r in range(value.shape[0]):
            row = plain_ref[pl.ds(r, 8, stride=0), :]
            vec_ref[r] = jnp.concatenate([row, row], axis=0).astype(BF16)

    def left_of(vec_ref, rows_out, base_in, base_out, g, i):
        value = vec_ref[index_ref[base_in + g, i]]
        value = jnp.concatenate([value] * (rows_out // 16), axis=0)
        goes = jnp.broadcast_to(goes_ref[base_out + g, i], (16, width)).astype(BF16)
        goes = jnp.concatenate([goes] * (rows_out // 16), axis=0)
        hot = iota((rows_out, width), 0).astype(F32).astype(BF16) == goes
        return jnp.where(hot, value, jnp.zeros_like(value))

    def feed(source, vec_ref, accs, base_in, base_out, g, t, q, register):
        tile = [source[g * width + t + i] for i in range(4)]
        right = jnp.concatenate(
            [jnp.concatenate(tile[:2], axis=1), jnp.concatenate(tile[2:], axis=1)], axis=0
        )
        rows_out = accs[0].shape[0]
        left = [left_of(vec_ref, rows_out, base_in, base_out, g, t + i) for i in range(4)]
        pltpu.matmul_push_rhs(right, staging_register=register, mxu_index=q)
        pltpu.matmul_acc_lhs(
            accs[2 * q], jnp.concatenate([left[0], left[2]], axis=1), load_staged_rhs=register
        )
        pltpu.matmul_acc_lhs(accs[2 * q + 1], jnp.concatenate([left[1], left[3]], axis=1))

    def feed_many(source, vec_ref, accs, base_in, base_out, g, t, pairs):
        for i in range(pairs):
            for q in range(2):
                feed(source, vec_ref, accs, base_in, base_out, g, t + 8 * i + 4 * q, q, i % 2)

    def taken(accs):
        pieces = [pltpu.matmul_pop(acc) for acc in accs]
        return (pieces[0][:, :width] + pieces[2][:, :width]) + (
            pieces[1][:, width:] + pieces[3][:, width:]
        )

    def full_pass(source, vec_ref, accs, base_in, base_out):
        @pl.loop(0, lines)
        def _(g):
            feed_many(source, vec_ref, accs, base_in, base_out, g, 0, width // 8)

        return taken(accs)

    def product(left_ref, right_of, use):
        high, deep = left_ref.shape
        for m in range(0, high, 2 * SIDE):
            for k in range(0, deep, SIDE):
                for p, right in enumerate(right_of(k)):
                    for q in range(2):
                        pltpu.matmul_push_rhs(right, staging_register=p % 2, mxu_index=q)
                        pltpu.matmul_acc_lhs(
                            acc_sum[q],
                            left_ref[pl.ds(m + q * SIDE, SIDE), pl.ds(k, SIDE)],
                            load_staged_rhs=p % 2,
                        )
            for q in range(2):
                use(m + q * SIDE, pltpu.matmul_pop(acc_sum[q]))

    def remote(source, target, sem, d):
        return pltpu.make_async_remote_copy(
            src_ref=source, dst_ref=target, send_sem=send_sem, recv_sem=sem,
            device_id=at(d), device_id_type=MESH,
        )

    def wait_for(ref, number, sem):
        ref = ref.at[pl.ds(0, number)]
        pltpu.make_async_copy(ref, ref, sem).wait()

    def total(x):
        return jnp.sum(x, keepdims=True)

    def send_keys():
        for k in range(QUARTERS):
            d = lax.rem(quarter + k, QUARTERS) * group + 2 * place + 1
            copy = remote(key_send, key_recv.at[which], key_sem, d)
            if k > 0:
                copy.start()
            else:
                pl.when(is_other)(copy.start)

    def send_sums(step):
        for k in range(chips - 1, -1, -1):
            to = chip ^ k if chips & (chips - 1) == 0 else lax.rem(chip + k, chips)
            d = 2 * to + 1
            copies = (
                remote(send_a.at[step, lax.rem(to, reducers)], recv_a.at[step, me], a_sem.at[step], d),
                remote(norm_a.at[step], norm_recv_a.at[step, me], na_sem.at[step], d),
            )

            def start(copies=copies):
                for copy in copies:
                    copy.start()

            if k > 0:
                start()
            else:
                pl.when(is_other)(start)

    def send_back(step, data):
        for k in range(group - 1, 0, -1):
            local = (
                lax.rem(me, group) ^ k if group & (group - 1) == 0 else lax.rem(me + k, group)
            )
            d = quarter * group + local
            if data:
                remote(send_b.at[step, local], recv_b.at[step, place], b_sem.at[step], d).start()
            remote(norm_b.at[step], norm_recv_b.at[step, place], nb_sem.at[step], d).start()

    def prepare():
        wait_for(key_recv, 2 * QUARTERS - 1, key_sem)
        key_recv[which] = key_send[...]
        row = jnp.sum(key_recv[...], axis=0)
        key_rows[...] = jnp.broadcast_to(row, key_rows.shape)
        for b in range(0, asked, width):
            block = key_rows[:, pl.ds(b, width)]
            column = jnp.concatenate([block] * (width // 8), axis=0).T
            times = jnp.zeros((width, width), F32)
            for c in range(0, asked, width):
                equal = jnp.where(column == key_rows[pl.ds(0, 1), pl.ds(c, width)], 1.0, 0.0)
                same_ref[pl.ds(b, width), pl.ds(c, width)] = equal.astype(BF16)
                times = times + equal
            times = jnp.sum(times, axis=1, keepdims=True)
            inv_ref[pl.ds(b, width), :] = jnp.broadcast_to(1.0 / times, (width, width))

    def prepare_out():
        first = (2 * quarter * BLK_DEV).astype(F32)
        high = out_hot.shape[0]
        number = iota((high, width), 0).astype(F32) + first
        for c in range(0, asked, width):
            equal = jnp.where(number == key_rows[pl.ds(0, 1), pl.ds(c, width)], 1.0, 0.0)
            out_hot[:, pl.ds(c, width)] = equal.astype(BF16)

    def turn():
        @pl.loop(0, count // 16)
        def _(g):
            for i in range(16):
                turned_ref[g * 16 + i] = tiles_ref[g * 16 + i].T

    u = None
    alpha = phibar = rhobar = None
    coefs = None
    uraw = rays_ref[...]
    for step in range(steps):
        if step > 0:
            spread_rows(cell_ref, recv_b[step - 1].reshape(slots_all, width).astype(F32))
            uraw = full_pass(turned_ref, cell_ref, acc_ray, lines, 0) / alpha - alpha * u
            spread_rows(ray_ref, uraw)
            sums = full_pass(tiles_ref, ray_ref, acc_cell, 0, lines)
        else:
            spread_rows(ray_ref, uraw)
            for copy in index_copies:
                copy.wait()
            per_line = width // per_chunk

            @pl.loop(0, lines)
            def _(g):
                for c in range(per_line):
                    tile_copy(g * per_line + c).wait()
                    feed_many(tiles_ref, ray_ref, acc_cell, 0, lines, g, c * per_chunk, per_chunk // 8)

            sums = taken(acc_cell)
        send_a[step] = sums.astype(BF16).reshape(reducers, part, width)
        norm_a[step] = jnp.sum(uraw * uraw, axis=0, keepdims=True)
        if step == 0:
            pl.when(is_reducer)(lambda: pl.semaphore_wait(barrier, n - 1))
            pl.when(is_other)(lambda: pl.semaphore_wait(barrier, chips))
            send_keys()
        send_sums(step)

        @pl.when(is_reducer)
        def _(step=step, alpha=alpha, phibar=phibar, rhobar=rhobar, coefs=coefs):
            recv_a[step, me] = send_a[step, place]
            norm_recv_a[step, me] = norm_a[step]
            if step == 0:
                prepare()
            else:
                v = vraw_ref[...] / alpha
                if step == 1:
                    w_ref[...] = v
                    update_ref[...] = jnp.zeros_like(v)
                else:
                    w = w_ref[...]
                    update_ref[...] = update_ref[...] + coefs[0] * w
                    w_ref[...] = v - coefs[1] * w
            if step == 1:
                prepare_out()

        if step == 0:
            turn()

        @pl.when(is_reducer)
        def _(step=step, alpha=alpha, phibar=phibar, rhobar=rhobar):
            wait_for(norm_recv_a.at[step], n - 1, na_sem.at[step])
            wait_for(recv_a.at[step], n - 1, a_sem.at[step])
            beta = jnp.sqrt(total(jnp.sum(norm_recv_a[step], axis=0)))

            def pieces(k):
                got = recv_a[step, pl.ds(k // part, SIDE // part)].reshape(SIDE, width)
                return (jnp.concatenate([got, got], axis=1),)

            squares = []

            def use(m, value):
                span = pl.ds(m, SIDE)
                vraw = value[:, :width] / beta
                if step > 0:
                    vraw = vraw - (beta / alpha) * vraw_ref[span, :]
                vraw_ref[span, :] = vraw
                squares.append(jnp.sum(vraw * vraw * inv_ref[span, :], axis=0, keepdims=True))

            product(same_ref, pieces, use)
            norm_b[step, pl.ds(0, 1), :] = functools.reduce(jnp.add, squares)
            norm_b[step, pl.ds(1, 1), :] = jnp.broadcast_to(beta, (1, width))
            if step < steps - 1:
                own = vraw_ref[pl.ds(pl.multiple_of(quarter * group * part, 8), group * part), :]
                send_b[step] = own.astype(BF16).reshape(group, part, width)
            send_back(step, step < steps - 1)
            norm_recv_b[step, place] = norm_b[step]
            if step < steps - 1:
                recv_b[step, place] = send_b[step, lax.rem(me, group)]
            else:
                rhobar1 = jnp.sqrt(rhobar * rhobar + damping * damping)
                rho = jnp.sqrt(rhobar1 * rhobar1 + beta * beta)
                scale = (rhobar1 / rho) * ((rhobar / rhobar1) * phibar) / rho
                update = (update_ref[...] + scale * w_ref[...]) * inv_ref[...]
                update_ref[...] = update
                vraw_ref[...] = vraw_ref[...] * inv_ref[...]

                def parts(k):
                    span = pl.ds(k, SIDE)
                    x = jnp.concatenate([update_ref[span, :], vraw_ref[span, :]], axis=1)
                    high = x.astype(BF16)
                    return high, (x - high.astype(F32)).astype(BF16)

                def use_final(m, value):
                    final_ref[m // SIDE] = value

                product(out_hot, parts, use_final)
                remote(final_ref.at[0], final_recv.at[0], final_sem, me - 1).start()
            wait_for(norm_recv_b.at[step], reducers - 1, nb_sem.at[step])
            if step < steps - 1:
                wait_for(recv_b.at[step], reducers - 1, b_sem.at[step])

        @pl.when(is_other)
        def _(step=step):
            wait_for(norm_recv_b.at[step], reducers, nb_sem.at[step])
            if step < steps - 1:
                wait_for(recv_b.at[step], reducers, b_sem.at[step])

        alpha = jnp.sqrt(total(jnp.sum(norm_recv_b[step], axis=0)[:1]))
        beta = norm_recv_b[step, 0, pl.ds(1, 1), pl.ds(0, 1)]
        u = uraw / beta
        if step == 0:
            phibar = beta
            rhobar = alpha
        else:
            rhobar1 = jnp.sqrt(rhobar * rhobar + damping * damping)
            phibar = rhobar / rhobar1 * phibar
            rho = jnp.sqrt(rhobar1 * rhobar1 + beta * beta)
            cosine = rhobar1 / rho
            sine = beta / rho
            theta = sine * alpha
            rhobar = -cosine * alpha
            phi = cosine * phibar
            phibar = sine * phibar
            coefs = (phi / rho, theta / rho)

    blocks = sol_ref.shape[0]
    scale = float(blocks * width * n) ** 0.5 / alpha

    def put(result):
        sol_ref[...] = result[:, :width]
        right_ref[...] = result[:, width:] * scale

    @pl.when(is_reducer)
    def _():
        put(final_ref[1])

    @pl.when(is_other)
    def _():
        wait_for(final_recv, 1, final_sem)
        put(final_recv[0])

    @pl.when(is_reducer)
    def _():
        for k in range(QUARTERS - 1):
            wait_for(key_recv, 1, send_sem)
        for step in range(steps):
            wait_for(recv_a.at[step], chips - 1, send_sem)
            wait_for(norm_recv_a.at[step], chips - 1, send_sem)
            wait_for(norm_b.at[pl.ds(0, 1)], 1, send_sem) if group == 2 else None
            for k in range(group - 1):
                wait_for(norm_recv_b.at[step], 1, send_sem)
                if step < steps - 1:
                    wait_for(recv_b.at[step], 1, send_sem)
        wait_for(final_recv, 1, send_sem)

    @pl.when(is_other)
    def _():
        for k in range(QUARTERS):
            wait_for(key_recv, 1, send_sem)
        for step in range(steps):
            wait_for(recv_a.at[step], chips, send_sem)
            wait_for(norm_recv_a.at[step], chips, send_sem)


def per_device(n, regs, tiles, rays, tile_rows, tile_slots, tile_count, wanted):
    count, width = tiles.shape[0], tiles.shape[2]
    cap = wanted.shape[2]
    steps = ITERS + 1
    row_blocks = rays.shape[0]
    group = n // QUARTERS
    reducers = group // 2
    part = 2 * QUARTERS * cap
    slots_all = n * cap
    asked = n * part
    lines = count // width
    vmem = pl.BlockSpec(memory_space=pltpu.VMEM)
    out = jax.ShapeDtypeStruct((BLK_DEV, width), F32)

    def body(*refs):
        def inner(acc_ray, acc_cell, acc_sum):
            kernel(n, regs, cap, *refs, acc_ray, acc_cell, acc_sum)

        def four(rows):
            return tuple(pltpu.ACC(q)((rows, SIDE), F32) for q in (0, 0, 1, 1))

        pl.run_scoped(
            inner, four(row_blocks), four(slots_all),
            tuple(pltpu.ACC(q)((SIDE, SIDE), F32) for q in (0, 1)),
        )

    return pl.pallas_call(
        body,
        out_shape=(out, out),
        in_specs=[vmem, pl.BlockSpec(memory_space=pl.ANY)] + [vmem] * 4,
        out_specs=(vmem, vmem),
        scratch_shapes=[
            pltpu.VMEM(tiles.shape, BF16),
            pltpu.VMEM(tiles.shape, BF16),
            pltpu.VMEM((2 * lines, width), jnp.int32),
            pltpu.SMEM((2 * lines, width), jnp.int32),
            pltpu.VMEM((2 * lines, width), F32),
            pltpu.SMEM((2 * lines, width), F32),
            pltpu.VMEM((max(row_blocks, slots_all) + 8, width), F32),
            pltpu.VMEM((row_blocks + 1, 16, width), BF16),
            pltpu.VMEM((slots_all + 1, 16, width), BF16),
            pltpu.VMEM((1, asked), F32),
            pltpu.VMEM((2 * QUARTERS, 1, asked), F32),
            pltpu.VMEM((8, asked), F32),
            pltpu.VMEM((asked, asked), BF16),
            pltpu.VMEM((2 * BLK_DEV, asked), BF16),
            pltpu.VMEM((asked, width), F32),
            pltpu.VMEM((asked, width), F32),
            pltpu.VMEM((asked, width), F32),
            pltpu.VMEM((asked, width), F32),
            pltpu.VMEM((2, BLK_DEV, 2 * width), F32),
            pltpu.VMEM((1, BLK_DEV, 2 * width), F32),
            pltpu.VMEM((steps, reducers, part, width), BF16),
            pltpu.VMEM((steps, n, part, width), BF16),
            pltpu.VMEM((steps, 1, width), F32),
            pltpu.VMEM((steps, n, 1, width), F32),
            pltpu.VMEM((steps - 1, group, part, width), BF16),
            pltpu.VMEM((steps - 1, reducers, part, width), BF16),
            pltpu.VMEM((steps, 2, width), F32),
            pltpu.VMEM((steps, reducers, 2, width), F32),
            pltpu.SemaphoreType.DMA((CHUNKS,)),
            pltpu.SemaphoreType.DMA((2,)),
            pltpu.SemaphoreType.DMA,
            pltpu.SemaphoreType.DMA,
            pltpu.SemaphoreType.DMA((steps,)),
            pltpu.SemaphoreType.DMA((steps,)),
            pltpu.SemaphoreType.DMA((steps,)),
            pltpu.SemaphoreType.DMA((steps,)),
            pltpu.SemaphoreType.DMA,
        ],
        compiler_params=pltpu.CompilerParams(
            collective_id=0, has_side_effects=True, vmem_limit_bytes=56 * 1024 * 1024
        ),
    )(
        tile_count[None, :],
        tiles,
        rays,
        tile_rows.reshape(lines, width),
        tile_slots.reshape(lines, width),
        wanted[0].T,
    )


def solution(mesh):
    both = ("src", "reg")
    in_specs = (
        P(both, None, None),
        P(both, None),
        P(both),
        P(both),
        P(both),
        P(both, None, None),
    )
    out_specs = (P(both, None), P(both, None))
    n = mesh.shape["src"] * mesh.shape["reg"]
    return jax.shard_map(
        functools.partial(per_device, n, mesh.shape["reg"]),
        mesh=mesh,
        in_specs=in_specs,
        out_specs=out_specs,
        check_vma=False,
    )
```

time: 79.5 us -> 65.9 us (0.83)
  Pallas kernels: 74.9 us -> 61.2 us
    pallas_call x1, Pallas kernels: 74.9 us -> 61.2 us  [per_device(): pl.pallas_call(body, out_shape=(out, out), in_specs=[vmem, pl.BlockSpec(m...]
where the time goes in v1:
time: 65.9 us; the launch traced here: 65.6 us
  Pallas kernels  61.2 us (93%)
  local copies, waits for them, and re-layouts  3.14 us (5%)
  between operations  1.29 us (2%)
    pallas_call x1, Pallas kernels, per_device(): pl.pallas_call(body, out_shape=(out, out), in_specs=[vmem, pl.BlockSpec(m...  61.2 us
    unnamed x2, local copies, waits for them, and re-layouts  3.14 us

profile of v1, /device:TPU:0, one launch (start us, length us, event | category | flops | bytes accessed | tf_op | source)
XLA Modules:
  0.0 65.6 jit_solution(8581638803807687551)
XLA Ops:
  1.3 61.2 %shard_map.77 = (f32[256,128]{1,0:T(8,128)}, f32[256,128]{1,0:T(8,128)}) custom-call(s32[1,1]{1,0:T(1,128)} %bitcast.6.refs_0_, bf16[512,128,128]{2,1,0:T(8,128)(2,1)} %refs_1_.1, f32[64,128]{1,0:T(8,128)} %refs_2_.1, s32[4,128]{1,0:T(4,128)} %bitcast.7, s32[4,128]{1,0:T(4,128)} %bitcast.8, s32[2,32]{1,0:T(2,128)} %bitcast.9), custom_call_target="tpu_custom_call" | custom-call | tf_op jit(solution)/shard_map/pallas_call | solution.py:454
  62.5 1.6 %copy.11 = f32[256,128]{1,0:T(8,128)} copy(f32[256,128]{1,0:T(8,128)} %get-tuple-element.4) | data formatting | bytes 262144
  64.1 1.6 %copy.12 = f32[256,128]{1,0:T(8,128)} copy(f32[256,128]{1,0:T(8,128)} %get-tuple-element.5) | data formatting | bytes 262144

commit v2 on v1

--- a/solution.py
+++ b/solution.py
@@ -13,6 +13,7 @@
 
 QUARTERS = 4
 CHUNKS = 16
+AHEAD = 6
 F32 = jnp.float32
 BF16 = jnp.bfloat16
 MESH = pl.DeviceIdType.MESH
@@ -21,13 +22,14 @@
 
 def kernel(
     n, regs, cap,
-    count_ref, tiles_hbm, rays_ref, rows_ref, slots_ref, wanted_ref,
-    sol_ref, right_ref,
+    count_hbm, tiles_hbm, rays_hbm, rows_hbm, slots_hbm, wanted_hbm,
+    result_ref,
+    count_ref, rays_ref, rows_ref, slots_ref, wanted_ref,
     tiles_ref, turned_ref, index_vec, index_ref, goes_vec, goes_ref, plain_ref, ray_ref, cell_ref,
     key_send, key_recv, key_rows, same_ref, out_hot, inv_ref,
     vraw_ref, w_ref, update_ref, final_ref, final_recv,
     send_a, recv_a, norm_a, norm_recv_a, send_b, recv_b, norm_b, norm_recv_b,
-    tile_sem, index_sem, send_sem, key_sem, a_sem, na_sem, b_sem, nb_sem, final_sem,
+    tile_sem, input_sem, index_sem, send_sem, key_sem, a_sem, na_sem, b_sem, nb_sem, final_sem,
     acc_ray, acc_cell, acc_sum,
 ):
     src = lax.axis_index("src")
@@ -56,7 +58,16 @@
         span = pl.ds(c * per_chunk, per_chunk)
         return pltpu.make_async_copy(tiles_hbm.at[span], tiles_ref.at[span], tile_sem.at[c])
 
-    for c in range(CHUNKS):
+    inputs = [
+        pltpu.make_async_copy(a, b, input_sem.at[i])
+        for i, (a, b) in enumerate((
+            (count_hbm, count_ref), (rows_hbm, rows_ref), (slots_hbm, slots_ref),
+            (rays_hbm, rays_ref), (wanted_hbm, wanted_ref),
+        ))
+    ]
+    for copy in inputs:
+        copy.start()
+    for c in range(AHEAD):
         tile_copy(c).start()
 
     def at(d):
@@ -81,9 +92,11 @@
     def _():
         greet(me + 1)
 
+    for copy in inputs:
+        copy.wait()
     lines = rows_ref.shape[0]
     tile_id = iota((lines, width), 0) * width + iota((lines, width), 1)
-    live = tile_id < count_ref[...]
+    live = tile_id < count_ref[0]
     slots = slots_ref[...]
     owner = slots // cap
     within = lax.rem(owner, group)
@@ -251,11 +264,16 @@
             equal = jnp.where(number == key_rows[pl.ds(0, 1), pl.ds(c, width)], 1.0, 0.0)
             out_hot[:, pl.ds(c, width)] = equal.astype(BF16)
 
-    def turn():
-        @pl.loop(0, count // 16)
-        def _(g):
-            for i in range(16):
-                turned_ref[g * 16 + i] = tiles_ref[g * 16 + i].T
+    early = per_chunk // 2
+
+    def turn(first, number):
+        for i in range(number):
+            turned_ref[first + i] = tiles_ref[first + i].T
+
+    def turn_rest():
+        @pl.loop(0, CHUNKS)
+        def _(c):
+            turn(c * per_chunk + early, per_chunk - early)
 
     u = None
     alpha = phibar = rhobar = None
@@ -273,20 +291,27 @@
                 copy.wait()
             per_line = width // per_chunk
 
-            @pl.loop(0, lines)
-            def _(g):
+            def line(g):
                 for c in range(per_line):
+                    if g * per_line + c + AHEAD < CHUNKS:
+                        tile_copy(g * per_line + c + AHEAD).start()
                     tile_copy(g * per_line + c).wait()
                     feed_many(tiles_ref, ray_ref, acc_cell, 0, lines, g, c * per_chunk, per_chunk // 8)
+                    turn((g * per_line + c) * per_chunk, early)
+
+            line(0)
+            pl.when(is_reducer)(lambda: pl.semaphore_wait(barrier, n - 1))
+            pl.when(is_other)(lambda: pl.semaphore_wait(barrier, chips))
+            send_keys()
+            for g in range(1, lines):
+                line(g)
 
             sums = taken(acc_cell)
         send_a[step] = sums.astype(BF16).reshape(reducers, part, width)
         norm_a[step] = jnp.sum(uraw * uraw, axis=0, keepdims=True)
+        send_sums(step)
         if step == 0:
-            pl.when(is_reducer)(lambda: pl.semaphore_wait(barrier, n - 1))
-            pl.when(is_other)(lambda: pl.semaphore_wait(barrier, chips))
-            send_keys()
-        send_sums(step)
+            turn_rest()
 
         @pl.when(is_reducer)
         def _(step=step, alpha=alpha, phibar=phibar, rhobar=rhobar, coefs=coefs):
@@ -306,9 +331,6 @@
             if step == 1:
                 prepare_out()
 
-        if step == 0:
-            turn()
-
         @pl.when(is_reducer)
         def _(step=step, alpha=alpha, phibar=phibar, rhobar=rhobar):
             wait_for(norm_recv_a.at[step], n - 1, na_sem.at[step])
@@ -386,12 +408,11 @@
             phibar = sine * phibar
             coefs = (phi / rho, theta / rho)
 
-    blocks = sol_ref.shape[0]
-    scale = float(blocks * width * n) ** 0.5 / alpha
+    scale = float(BLK_DEV * width * n) ** 0.5 / alpha
 
     def put(result):
-        sol_ref[...] = result[:, :width]
-        right_ref[...] = result[:, width:] * scale
+        result_ref[pl.ds(0, BLK_DEV), :] = result[:, :width]
+        result_ref[pl.ds(BLK_DEV, BLK_DEV), :] = result[:, width:] * scale
 
     @pl.when(is_reducer)
     def _():
@@ -437,7 +458,7 @@
     asked = n * part
     lines = count // width
     vmem = pl.BlockSpec(memory_space=pltpu.VMEM)
-    out = jax.ShapeDtypeStruct((BLK_DEV, width), F32)
+    out = jax.ShapeDtypeStruct((2 * BLK_DEV, width), F32)
 
     def body(*refs):
         def inner(acc_ray, acc_cell, acc_sum):
@@ -451,12 +472,17 @@
             tuple(pltpu.ACC(q)((SIDE, SIDE), F32) for q in (0, 1)),
         )
 
-    return pl.pallas_call(
+    result = pl.pallas_call(
         body,
-        out_shape=(out, out),
-        in_specs=[vmem, pl.BlockSpec(memory_space=pl.ANY)] + [vmem] * 4,
-        out_specs=(vmem, vmem),
+        out_shape=out,
+        in_specs=[pl.BlockSpec(memory_space=pl.ANY)] * 6,
+        out_specs=vmem,
         scratch_shapes=[
+            pltpu.SMEM((1,), jnp.int32),
+            pltpu.VMEM(rays.shape, F32),
+            pltpu.VMEM((lines, width), jnp.int32),
+            pltpu.VMEM((lines, width), jnp.int32),
+            pltpu.VMEM((cap, n), jnp.int32),
             pltpu.VMEM(tiles.shape, BF16),
             pltpu.VMEM(tiles.shape, BF16),
             pltpu.VMEM((2 * lines, width), jnp.int32),
@@ -486,6 +512,7 @@
             pltpu.VMEM((steps, 2, width), F32),
             pltpu.VMEM((steps, reducers, 2, width), F32),
             pltpu.SemaphoreType.DMA((CHUNKS,)),
+            pltpu.SemaphoreType.DMA((5,)),
             pltpu.SemaphoreType.DMA((2,)),
             pltpu.SemaphoreType.DMA,
             pltpu.SemaphoreType.DMA,
@@ -499,13 +526,14 @@
             collective_id=0, has_side_effects=True, vmem_limit_bytes=56 * 1024 * 1024
         ),
     )(
-        tile_count[None, :],
+        tile_count,
         tiles,
         rays,
         tile_rows.reshape(lines, width),
         tile_slots.reshape(lines, width),
         wanted[0].T,
     )
+    return result[:BLK_DEV], result[BLK_DEV:]
 
 
 def solution(mesh):

time: 65.9 us -> 59.2 us (0.90)
  Pallas kernels: 61.2 us -> 56.1 us
  local copies, waits for them, and re-layouts: 3.14 us -> 1.69 us
    pallas_call x1, Pallas kernels: 61.2 us -> 56.1 us  [per_device(): pl.pallas_call(body, out_shape=out, in_specs=[pl.BlockSpec(memory_space=p...]
    unnamed x2 -> x0, local copies, waits for them, and re-layouts: 3.14 us -> none
    slice x0 -> x1, local copies, waits for them, and re-layouts: none -> 1.69 us  [per_device(): return (result[:BLK_DEV], result[BLK_DEV:])]
where the time goes in v2:
time: 59.2 us; the launch traced here: 59 us
  Pallas kernels  56.1 us (95%)
  local copies, waits for them, and re-layouts  1.69 us (3%)
  between operations  1.29 us (2%)
    pallas_call x1, Pallas kernels, per_device(): pl.pallas_call(body, out_shape=out, in_specs=[pl.BlockSpec(memory_space=p...  56.1 us
    slice x1, local copies, waits for them, and re-layouts, per_device(): return (result[:BLK_DEV], result[BLK_DEV:])  1.69 us

profile of v2, /device:TPU:0, one launch (start us, length us, event | category | flops | bytes accessed | tf_op | source)
XLA Modules:
  0.0 59.0 jit_solution(9197988981282031295)
XLA Ops:
  1.3 56.1 %shard_map.77 = f32[512,128]{1,0:T(8,128)} custom-call(s32[1]{0:T(128)S(6)} %copy.8.refs_0_, bf16[512,128,128]{2,1,0:T(8,128)(2,1)} %refs_1_.1, f32[64,128]{1,0:T(8,128)} %refs_2_.1, s32[4,128]{1,0:T(4,128)} %bitcast.5, s32[4,128]{1,0:T(4,128)} %bitcast.6, s32[2,32]{1,0:T(2,128)} %bitcast.7), custom_call_target="tpu_custom_call" | custom-call | tf_op jit(solution)/shard_map/pallas_call | solution.py:475
  57.4 1.7 %fusion = (f32[256,128]{1,0:T(8,128)}, f32[256,128]{1,0:T(8,128)}) fusion(f32[512,128]{1,0:T(8,128)} %shard_map.77), kind=kLoop, calls=%fused_computation | loop fusion | bytes 524288 | tf_op jit(solution)/shard_map/slice | solution.py:536

commit v3 on v2

--- a/solution.py
+++ b/solution.py
@@ -168,27 +168,29 @@
             pieces[1][:, width:] + pieces[3][:, width:]
         )
 
-    def full_pass(source, vec_ref, accs, base_in, base_out):
-        @pl.loop(0, lines)
-        def _(g):
+    def full_pass(source, vec_ref, accs, base_in, base_out, late=None):
+        for g in range(lines):
+            if late is not None and g == lines - 1:
+                late()
             feed_many(source, vec_ref, accs, base_in, base_out, g, 0, width // 8)
 
         return taken(accs)
 
-    def product(left_ref, right_of, use):
-        high, deep = left_ref.shape
-        for m in range(0, high, 2 * SIDE):
+    def product(left_ref, right_of, use, accs=acc_sum, first=0, high=None):
+        deep = left_ref.shape[1]
+        high = left_ref.shape[0] if high is None else high
+        tall = accs[0].shape[0]
+        for m in range(0, high, 2 * tall):
             for k in range(0, deep, SIDE):
                 for p, right in enumerate(right_of(k)):
                     for q in range(2):
+                        span = pl.ds(pl.multiple_of(first + m + q * tall, 16), tall)
                         pltpu.matmul_push_rhs(right, staging_register=p % 2, mxu_index=q)
                         pltpu.matmul_acc_lhs(
-                            acc_sum[q],
-                            left_ref[pl.ds(m + q * SIDE, SIDE), pl.ds(k, SIDE)],
-                            load_staged_rhs=p % 2,
+                            accs[q], left_ref[span, pl.ds(k, SIDE)], load_staged_rhs=p % 2
                         )
             for q in range(2):
-                use(m + q * SIDE, pltpu.matmul_pop(acc_sum[q]))
+                use(m + q * tall, pltpu.matmul_pop(accs[q]))
 
     def remote(source, target, sem, d):
         return pltpu.make_async_remote_copy(
@@ -212,33 +214,30 @@
             else:
                 pl.when(is_other)(copy.start)
 
-    def send_sums(step):
+    def send_sums(step, norms):
         for k in range(chips - 1, -1, -1):
             to = chip ^ k if chips & (chips - 1) == 0 else lax.rem(chip + k, chips)
             d = 2 * to + 1
-            copies = (
-                remote(send_a.at[step, lax.rem(to, reducers)], recv_a.at[step, me], a_sem.at[step], d),
-                remote(norm_a.at[step], norm_recv_a.at[step, me], na_sem.at[step], d),
-            )
-
-            def start(copies=copies):
-                for copy in copies:
-                    copy.start()
-
+            if norms:
+                copy = remote(norm_a.at[step], norm_recv_a.at[step, me], na_sem.at[step], d)
+            else:
+                source = send_a.at[step, lax.rem(to, reducers)]
+                copy = remote(source, recv_a.at[step, me], a_sem.at[step], d)
             if k > 0:
-                start()
-            else:
-                pl.when(is_other)(start)
-
-    def send_back(step, data):
+                copy.start()
+            else:
+                pl.when(is_other)(copy.start)
+
+    def send_back(step, norms):
         for k in range(group - 1, 0, -1):
             local = (
                 lax.rem(me, group) ^ k if group & (group - 1) == 0 else lax.rem(me + k, group)
             )
             d = quarter * group + local
-            if data:
+            if norms:
+                remote(norm_b.at[step], norm_recv_b.at[step, place], nb_sem.at[step], d).start()
+            else:
                 remote(send_b.at[step, local], recv_b.at[step, place], b_sem.at[step], d).start()
-            remote(norm_b.at[step], norm_recv_b.at[step, place], nb_sem.at[step], d).start()
 
     def prepare():
         wait_for(key_recv, 2 * QUARTERS - 1, key_sem)
@@ -275,17 +274,47 @@
         def _(c):
             turn(c * per_chunk + early, per_chunk - early)
 
-    u = None
+    def wait_norms(step):
+        @pl.when(is_reducer)
+        def _():
+            wait_for(norm_recv_b.at[step], reducers - 1, nb_sem.at[step])
+
+        @pl.when(is_other)
+        def _():
+            wait_for(norm_recv_b.at[step], reducers, nb_sem.at[step])
+
     alpha = phibar = rhobar = None
     coefs = None
     uraw = rays_ref[...]
     for step in range(steps):
         if step > 0:
             spread_rows(cell_ref, recv_b[step - 1].reshape(slots_all, width).astype(F32))
-            uraw = full_pass(turned_ref, cell_ref, acc_ray, lines, 0) / alpha - alpha * u
+            forward = full_pass(
+                turned_ref, cell_ref, acc_ray, lines, 0, functools.partial(wait_norms, step - 1)
+            )
+            alpha = jnp.sqrt(total(jnp.sum(norm_recv_b[step - 1], axis=0)[:1]))
+            beta = norm_recv_b[step - 1, 0, pl.ds(1, 1), pl.ds(0, 1)]
+            if step == 1:
+                phibar = beta
+                rhobar = alpha
+            else:
+                rhobar1 = jnp.sqrt(rhobar * rhobar + damping * damping)
+                phibar = rhobar / rhobar1 * phibar
+                rho = jnp.sqrt(rhobar1 * rhobar1 + beta * beta)
+                cosine = rhobar1 / rho
+                sine = beta / rho
+                theta = sine * alpha
+                rhobar = -cosine * alpha
+                phi = cosine * phibar
+                phibar = sine * phibar
+                coefs = (phi / rho, theta / rho)
+            uraw = forward * (1.0 / alpha) - (alpha / beta) * uraw
+            norm_a[step] = jnp.sum(uraw * uraw, axis=0, keepdims=True)
+            send_sums(step, True)
             spread_rows(ray_ref, uraw)
             sums = full_pass(tiles_ref, ray_ref, acc_cell, 0, lines)
         else:
+            norm_a[step] = jnp.sum(uraw * uraw, axis=0, keepdims=True)
             spread_rows(ray_ref, uraw)
             for copy in index_copies:
                 copy.wait()
@@ -303,13 +332,12 @@
             pl.when(is_reducer)(lambda: pl.semaphore_wait(barrier, n - 1))
             pl.when(is_other)(lambda: pl.semaphore_wait(barrier, chips))
             send_keys()
+            send_sums(step, True)
             for g in range(1, lines):
                 line(g)
-
             sums = taken(acc_cell)
         send_a[step] = sums.astype(BF16).reshape(reducers, part, width)
-        norm_a[step] = jnp.sum(uraw * uraw, axis=0, keepdims=True)
-        send_sums(step)
+        send_sums(step, False)
         if step == 0:
             turn_rest()
 
@@ -330,37 +358,53 @@
                     w_ref[...] = v - coefs[1] * w
             if step == 1:
                 prepare_out()
-
-        @pl.when(is_reducer)
-        def _(step=step, alpha=alpha, phibar=phibar, rhobar=rhobar):
             wait_for(norm_recv_a.at[step], n - 1, na_sem.at[step])
+            beta = jnp.sqrt(total(jnp.sum(norm_recv_a[step], axis=0)))
+            over = 1.0 / beta
+            back = None if step == 0 else beta / alpha
             wait_for(recv_a.at[step], n - 1, a_sem.at[step])
-            beta = jnp.sqrt(total(jnp.sum(norm_recv_a[step], axis=0)))
 
             def pieces(k):
                 got = recv_a[step, pl.ds(k // part, SIDE // part)].reshape(SIDE, width)
                 return (jnp.concatenate([got, got], axis=1),)
 
+            def vraw_of(span, value):
+                vraw = value[:, :width] * over
+                if step > 0:
+                    vraw = vraw - back * vraw_ref[span, :]
+                return vraw
+
+            if step < steps - 1:
+                tall = acc_ray[0].shape[0]
+                own = quarter * group * part
+
+                def use_own(m, value):
+                    span = pl.ds(pl.multiple_of(own + m, 16), tall)
+                    vraw = vraw_of(span, value).astype(BF16)
+                    send_b[step, pl.ds(m // part, tall // part)] = vraw.reshape(
+                        tall // part, part, width
+                    )
+
+                product(
+                    same_ref, pieces, use_own, (acc_ray[0], acc_ray[2]), own, group * part
+                )
+                send_back(step, False)
             squares = []
 
             def use(m, value):
                 span = pl.ds(m, SIDE)
-                vraw = value[:, :width] / beta
-                if step > 0:
-                    vraw = vraw - (beta / alpha) * vraw_ref[span, :]
+                vraw = vraw_of(span, value)
                 vraw_ref[span, :] = vraw
                 squares.append(jnp.sum(vraw * vraw * inv_ref[span, :], axis=0, keepdims=True))
 
             product(same_ref, pieces, use)
             norm_b[step, pl.ds(0, 1), :] = functools.reduce(jnp.add, squares)
             norm_b[step, pl.ds(1, 1), :] = jnp.broadcast_to(beta, (1, width))
-            if step < steps - 1:
-                own = vraw_ref[pl.ds(pl.multiple_of(quarter * group * part, 8), group * part), :]
-                send_b[step] = own.astype(BF16).reshape(group, part, width)
-            send_back(step, step < steps - 1)
+            send_back(step, True)
             norm_recv_b[step, place] = norm_b[step]
             if step < steps - 1:
                 recv_b[step, place] = send_b[step, lax.rem(me, group)]
+                wait_for(recv_b.at[step], reducers - 1, b_sem.at[step])
             else:
                 rhobar1 = jnp.sqrt(rhobar * rhobar + damping * damping)
                 rho = jnp.sqrt(rhobar1 * rhobar1 + beta * beta)
@@ -380,34 +424,15 @@
 
                 product(out_hot, parts, use_final)
                 remote(final_ref.at[0], final_recv.at[0], final_sem, me - 1).start()
-            wait_for(norm_recv_b.at[step], reducers - 1, nb_sem.at[step])
-            if step < steps - 1:
-                wait_for(recv_b.at[step], reducers - 1, b_sem.at[step])
-
-        @pl.when(is_other)
-        def _(step=step):
-            wait_for(norm_recv_b.at[step], reducers, nb_sem.at[step])
-            if step < steps - 1:
+
+        if step < steps - 1:
+
+            @pl.when(is_other)
+            def _(step=step):
                 wait_for(recv_b.at[step], reducers, b_sem.at[step])
 
-        alpha = jnp.sqrt(total(jnp.sum(norm_recv_b[step], axis=0)[:1]))
-        beta = norm_recv_b[step, 0, pl.ds(1, 1), pl.ds(0, 1)]
-        u = uraw / beta
-        if step == 0:
-            phibar = beta
-            rhobar = alpha
-        else:
-            rhobar1 = jnp.sqrt(rhobar * rhobar + damping * damping)
-            phibar = rhobar / rhobar1 * phibar
-            rho = jnp.sqrt(rhobar1 * rhobar1 + beta * beta)
-            cosine = rhobar1 / rho
-            sine = beta / rho
-            theta = sine * alpha
-            rhobar = -cosine * alpha
-            phi = cosine * phibar
-            phibar = sine * phibar
-            coefs = (phi / rho, theta / rho)
-
+    wait_norms(steps - 1)
+    alpha = jnp.sqrt(total(jnp.sum(norm_recv_b[steps - 1], axis=0)[:1]))
     scale = float(BLK_DEV * width * n) ** 0.5 / alpha
 
     def put(result):
@@ -430,7 +455,6 @@
         for step in range(steps):
             wait_for(recv_a.at[step], chips - 1, send_sem)
             wait_for(norm_recv_a.at[step], chips - 1, send_sem)
-            wait_for(norm_b.at[pl.ds(0, 1)], 1, send_sem) if group == 2 else None
             for k in range(group - 1):
                 wait_for(norm_recv_b.at[step], 1, send_sem)
                 if step < steps - 1:
@@ -474,7 +498,7 @@
 
     result = pl.pallas_call(
         body,
-        out_shape=out,
+        out_shape=pltpu.VMEM((2 * BLK_DEV, width), F32),
         in_specs=[pl.BlockSpec(memory_space=pl.ANY)] * 6,
         out_specs=vmem,
         scratch_shapes=[

time: 59.2 us -> 55.2 us (0.932)
  Pallas kernels: 56.1 us -> 53.1 us
  local copies, waits for them, and re-layouts: 1.69 us -> 0.72 us
    pallas_call x1, Pallas kernels: 56.1 us -> 53.1 us  [per_device(): pl.pallas_call(body, out_shape=pltpu.VMEM((2 * BLK_DEV, width), F32), in_...]
    slice x1, local copies, waits for them, and re-layouts: 1.69 us -> 0.72 us  [per_device(): return (result[:BLK_DEV], result[BLK_DEV:])]
where the time goes in v3:
time: 55.2 us; the launch traced here: 55.1 us
  Pallas kernels  53.1 us (96%)
  between operations  1.29 us (2%)
  local copies, waits for them, and re-layouts  0.72 us (1%)
    pallas_call x1, Pallas kernels, per_device(): pl.pallas_call(body, out_shape=pltpu.VMEM((2 * BLK_DEV, width), F32), in_...  53.1 us

profile of v3, /device:TPU:0, one launch (start us, length us, event | category | flops | bytes accessed | tf_op | source)
XLA Modules:
  0.0 55.1 jit_solution(13775791919077811808)
XLA Ops:
  1.3 53.1 %shard_map.77 = f32[512,128]{1,0:T(8,128)S(1)} custom-call(s32[1]{0:T(128)S(6)} %copy.8.refs_0_, bf16[512,128,128]{2,1,0:T(8,128)(2,1)} %refs_1_.1, f32[64,128]{1,0:T(8,128)} %refs_2_.1, s32[4,128]{1,0:T(4,128)} %bitcast.5, s32[4,128]{1,0:T(4,128)} %bitcast.6, s32[2,32]{1,0:T(2,128)} %bitcast.7), custom_call_target="tpu_custom_call" | custom-call | tf_op jit(solution)/shard_map/pallas_call | solution.py:499
  54.4 0.7 %fusion = (f32[256,128]{1,0:T(8,128)}, f32[256,128]{1,0:T(8,128)}) fusion(f32[512,128]{1,0:T(8,128)S(1)} %shard_map.77), kind=kLoop, calls=%fused_computation | loop fusion | bytes 524288 | tf_op jit(solution)/shard_map/slice | solution.py:560
